TPU v7x, 128 devices: a whole 4x4x4 slice. The times are simulated.
128 devices in a mesh: tp: 4 (over x_hi, core), grp: 32 (over z, x_lo, y).
Axes of the slice: x: 4 (x_hi: 2, x_lo: 2; x = x_hi * 2 + x_lo), y: 4, z: 4, core: 2. Of those that a mesh axis runs over, the one named last changes fastest.
Arguments:
- flat_shards: bfloat16 [2, 2, 8448, 24576], P(None, None, ('grp', 'tp')), may hold values from -0.0625 to 0.0625
- offsets: int32 [2, 2], replicated, may hold values from 0 to 2
- probes: bfloat16 [512, 8192], P(None, 'grp'), may hold values from -6 to 6
Outputs:
- serving_tiles: bfloat16 [2, 2, 8192, 24576], P(None, None, 'grp', 'tp')
- hidden_check: bfloat16 [2, 512, 24576], P(None, 'grp', 'tp')
All inputs are finite; a program needn't handle non-finite values.
Results may differ from a plain program's by a relative error of at most 0.001.
Values may be sent and summed in bfloat16 or wider, within the bound.
A program may use at most 320 MiB of HBM per device.

v0:
```python
import jax
import jax.numpy as jnp
from jax import lax
from jax.sharding import PartitionSpec as P

PAD = 2


def per_device(flat_shards, offsets, probes):
    tp_count = lax.axis_size("tp")
    grp_count = lax.axis_size("grp")
    layer_count = flat_shards.shape[0]
    shard_rows = flat_shards.shape[2] - PAD
    width = flat_shards.shape[3]
    columns = width // tp_count
    picked_list = []
    for which_layer in range(layer_count):
        for which_tensor in range(2):
            start = offsets[which_layer, which_tensor]
            picked_list.append(
                lax.dynamic_slice_in_dim(
                    flat_shards[which_layer, which_tensor], start, shard_rows, 0
                )
            )
    picked = jnp.stack(picked_list).reshape(layer_count, 2, 1, shard_rows, tp_count, columns)
    moved = lax.all_to_all(picked, "tp", split_axis=4, concat_axis=2, tiled=True)
    serving_tiles = moved.reshape(layer_count, 2, tp_count * shard_rows, columns)
    sub_cols = columns // grp_count
    split_tiles = serving_tiles.reshape(layer_count, 2, serving_tiles.shape[2], grp_count, sub_cols)
    column_tiles = lax.all_to_all(split_tiles, "grp", split_axis=3, concat_axis=2, tiled=True)
    column_tiles = column_tiles.reshape(layer_count, 2, column_tiles.shape[2], sub_cols)
    all_probes = lax.all_gather(probes, "grp", axis=1, tiled=True)
    sums = jnp.einsum("md,lkdc->mlkc", all_probes, column_tiles, preferred_element_type=jnp.float32)
    gated = (jax.nn.silu(sums[:, :, 0]) * sums[:, :, 1]).astype(jnp.bfloat16)
    returned = lax.all_to_all(gated, "grp", split_axis=0, concat_axis=2, tiled=True)
    hidden_check = jnp.transpose(returned, (1, 0, 2))
    return (serving_tiles, hidden_check)


def solution(mesh):
    placed = (P(None, None, ("grp", "tp"), None), P(), P(None, "grp"))
    return jax.shard_map(
        per_device,
        mesh=mesh,
        in_specs=placed,
        out_specs=(P(None, None, "grp", "tp"), P(None, "grp", "tp")),
        check_vma=False,
    )
```

profile of v0, /device:TPU:0, one launch (start us, length us, event | category | flops | bytes accessed | tf_op | source)
XLA Modules:
  0.0 650.1 jit_solution(928571724292559742)
XLA Ops:
  7.2 1.4 fusion.8
  13.4 30.7 %fusion.7 = (bf16[1,1,66,24576]{3,1,2,0:T(2,128)(2,1)}, bf16[1,1,66,24576]{3,1,2,0:T(2,128)(2,1)}, bf16[1,1,66,24576]{3,1,2,0:T(2,128)(2,1)}, bf16[1,1,66,24576]{3,1,2,0:T(2,128)(2,1)}) fusion(bf16[2,2,66,24576]{3,1,2,0:T(2,128)(2,1)} %param.3), kind=kLoop, calls=%fused_computation.17 | loop fusion | bytes 25952256 | tf_op jit(solution)/shard_map/slice | solution.py:22
  45.3 14.5 %constant_dynamic-slice_fusion.2 = (bf16[1,1,64,24576]{3,1,2,0:T(2,128)(2,1)S(1)}, bf16[1,1,64,24576]{3,1,2,0:T(2,128)(2,1)S(1)}) fusion(bf16[1,1,66,24576]{3,1,2,0:T(2,128)(2,1)} %get-tuple-element.4, s32[]{:T(128)S(6)} %select_n.13, bf16[1,1,66,24576]{3,1,2,0:T(2,128)(2,1)} %get-tuple-element.2, s32[]{:T(128)S(6)} %select_n.12), kind=kLoop, calls=%fused_computation.14 | loop fusion | bytes 12582920 | tf_op jit(solution)/shard_map/dynamic_slice | solution.py:21
  59.8 3.4 copy.55
  63.2 5.1 copy.56
  69.4 14.7 %constant_dynamic-slice_fusion = (bf16[1,1,64,24576]{3,1,2,0:T(2,128)(2,1)S(1)}, bf16[1,1,64,24576]{3,1,2,0:T(2,128)(2,1)S(1)}) fusion(bf16[1,1,66,24576]{3,1,2,0:T(2,128)(2,1)} %get-tuple-element.5, s32[]{:T(128)S(6)} %select_n.15, bf16[1,1,66,24576]{3,1,2,0:T(2,128)(2,1)} %get-tuple-element.3, s32[]{:T(128)S(6)} %select_n.14), kind=kLoop, calls=%fused_computation.12 | loop fusion | bytes 12582920 | tf_op jit(solution)/shard_map/dynamic_slice | solution.py:21
  84.1 3.4 copy.53
  87.5 0.0 copy-start
  87.5 3.4 copy.54
  90.9 0.0 copy-done
  90.9 5.5 pad_maximum_fusion
  96.4 17.8 %reshape.24 = bf16[2,2,1,64,4,6144]{5,4,3,1,0,2:T(4,128)(2,1)} reshape(bf16[4,64,24576]{2,1,0:T(8,128)(2,1)} %pad_maximum_fusion) | data formatting | bytes 25165824 | tf_op jit(solution)/shard_map/reshape | solution.py:25
  114.1 14.5 %copy.29 = bf16[2,2,1,64,4,6144]{5,3,1,0,2,4:T(8,128)(2,1)} copy(bf16[2,2,1,64,4,6144]{5,4,3,1,0,2:T(4,128)(2,1)} %reshape.24) | data formatting | bytes 25165824 | tf_op jit(solution)/shard_map/reshape | solution.py:25
  128.6 6.3 all-to-all-start
  135.0 0.0 all-gather.2.cloned.1.call-start
  135.0 0.7 all-gather.2.cloned.1.call-update
  135.7 224.2 %all-to-all-done = bf16[2,2,1,64,4,6144]{5,3,1,0,2,4:T(8,128)(2,1)} async-done(((bf16[2,2,1,64,4,6144]{5,3,1,0,2,4:T(8,128)(2,1)}), bf16[2,2,1,64,4,6144]{5,3,1,0,2,4:T(8,128)(2,1)}, u32[]{:S(2)}, u32[]{:S(2)}) %all-to-all-start) | async-done | bytes 12582944 | tf_op jit(solution)/shard_map/all_to_all | solution.py:26
  359.9 10.8 %copy.57 = bf16[2,2,1,64,4,6144]{5,3,4,1,0,2:T(8,128)(2,1)} copy(bf16[2,2,1,64,4,6144]{5,3,1,0,2,4:T(8,128)(2,1)} %all-to-all-done) | data formatting | bytes 25165824 | tf_op jit(solution)/shard_map/all_to_all | solution.py:26
  370.7 27.6 %reshape_reshape.3 = bf16[2,2,256,32,192]{4,3,2,1,0:T(8,128)(2,1)} reshape(bf16[2,2,4,1,64,1,6144]{6,4,2,1,0,5,3:T(8,128)(2,1)} %bitcast.64) | data formatting | bytes 25165824 | tf_op jit(solution)/shard_map/reshape;reshape | solution.py:29
  398.2 27.4 %copy.31 = bf16[2,2,256,32,192]{2,4,1,0,3:T(8,128)(2,1)} copy(bf16[2,2,256,32,192]{4,3,2,1,0:T(8,128)(2,1)} %reshape_reshape.3) | data formatting | bytes 25165824 | tf_op jit(solution)/shard_map/reshape;reshape | solution.py:29
  425.6 150.6 %all_to_all.48 = bf16[2,2,256,32,192]{2,4,1,0,3:T(8,128)(2,1)S(1)} all-to-all(bf16[2,2,256,32,192]{2,4,1,0,3:T(8,128)(2,1)} %copy.31), channel_id=1, replica_groups=mesh['tp'=4,'grp'=32] {'grp'}, dimensions={3} | all-to-all | bytes 25165824 | tf_op jit(solution)/shard_map/all_to_all | solution.py:30
  576.2 17.2 %copy.32 = bf16[2,2,32,256,1,192]{3,2,5,1,0,4:T(8,128)(2,1)} copy(bf16[2,2,32,256,1,192]{3,5,1,0,2,4:T(8,128)(2,1)S(1)} %bitcast.66) | data formatting | bytes 25165824 | tf_op jit(solution)/shard_map/all_to_all | solution.py:30
  593.4 19.5 %reshape.26 = bf16[2,2,8192,192]{2,3,1,0:T(8,128)(2,1)} reshape(bf16[2,2,32,256,1,192]{3,2,5,1,0,4:T(8,128)(2,1)} %copy.32) | data formatting | bytes 25165824 | tf_op jit(solution)/shard_map/reshape | solution.py:31
  612.9 0.0 all-gather.2.cloned.1.call-done
  612.9 11.8 %fusion.2 = f32[512,2,2,192]{0,3,2,1:T(8,128)S(1)} fusion(bf16[2,2,8192,192]{2,3,1,0:T(8,128)(2,1)} %reshape.26, bf16[512,8192]{1,0:T(8,128)(2,1)} %all-gather.2.cloned.1.call-done), kind=kOutput, calls=%fused_computation.7 | convolution fusion | flops 6442450944 | bytes 22544384 | tf_op jit(solution)/shard_map/md,lkdc->mlkc/dot_general | solution.py:33
  624.7 0.2 fusion.6
  625.0 0.4 copy.34
  625.4 16.2 %all_to_all.49 = bf16[512,2,192]{2,1,0:T(2,128)(2,1)S(1)} all-to-all(bf16[512,2,192]{2,1,0:T(2,128)(2,1)S(1)} %copy.34), channel_id=1, replica_groups=mesh['tp'=4,'grp'=32] {'grp'}, dimensions={0} | all-to-all | bytes 786432 | tf_op jit(solution)/shard_map/all_to_all | solution.py:35
  641.7 0.1 copy.35
  641.8 0.2 copy.36
  641.9 1.3 all_to_all.44
Async XLA Ops:
  87.5 3.4 copy-start
  128.6 231.2 %all-to-all-start = ((bf16[2,2,1,64,4,6144]{5,3,1,0,2,4:T(8,128)(2,1)}), bf16[2,2,1,64,4,6144]{5,3,1,0,2,4:T(8,128)(2,1)}, u32[]{:S(2)}, u32[]{:S(2)}) async-start(bf16[2,2,1,64,4,6144]{5,3,1,0,2,4:T(8,128)(2,1)} %copy.29), calls=%async_computation | async-start | bytes 25165824 | tf_op jit(solution)/shard_map/all_to_all | solution.py:26
  135.0 478.0 %all-gather.2.cloned.1.call-start = ((), (), s32[]{:S(2)}) async-start(), calls=%async_computation.3 | async-start | bytes 8650752 | tf_op jit(solution)/shard_map/all_gather | solution.py:32
Sparse Core Ops, SparseCore 0:
  137.3 228.1 all-gather.1
where the time goes:
time: 653 us; the launch traced here: 650 us
  waiting for transfers between devices  225 us (34%)
  local copies, waits for them, and re-layouts  213 us (33%)
  blocking collectives  167 us (26%)
  between operations  21.3 us (3%)
  matrix products  11.8 us (2%)
    all_to_all x1, waiting for transfers between devices, per_device(): lax.all_to_all(picked, 'tp', split_axis=4, concat_axis=2, tiled=True)  224 us
    all_to_all x1, blocking collectives, per_device(): lax.all_to_all(split_tiles, 'grp', split_axis=3, concat_axis=2, tiled=True)  151 us
    another operation x2, local copies, waits for them, and re-layouts, per_device(): serving_tiles.reshape(layer_count, 2, serving_tiles.shape[2], grp_count,...  54.9 us
    reshape x2, local copies, waits for them, and re-layouts, per_device(): jnp.stack(picked_list)  32.3 us
    slice x1, local copies, waits for them, and re-layouts, per_device(): flat_shards[which_layer, which_tensor]  30.7 us
    dynamic_slice x2, local copies, waits for them, and re-layouts, per_device(): lax.dynamic_slice_in_dim(flat_shards[which_layer, which_tensor], start, s...  29.2 us
    reshape x1, local copies, waits for them, and re-layouts, per_device(): column_tiles.reshape(layer_count, 2, column_tiles.shape[2], sub_cols)  19.5 us
    all_to_all x1, local copies, waits for them, and re-layouts, per_device(): lax.all_to_all(split_tiles, 'grp', split_axis=3, concat_axis=2, tiled=True)  17.2 us
  transfers between devices with their start and end apart: 2, of which 1 were waited for; matrix products, arithmetic and copies ran while one was open for 16% of the time, Pallas kernels for 0%

commit v1 on v0

v1 whole, which is shorter than its diff:
```python
import functools

import jax
import jax.numpy as jnp
from jax import lax
from jax.experimental import pallas as pl
from jax.experimental.pallas import tpu as pltpu
from jax.sharding import PartitionSpec as P

PAD = 2
LANES = 128
N_Y = 4
N_Z = 4
N_Q = N_Y * N_Z
STAGES = 4
MESH = pl.DeviceIdType.MESH

STEPS = (
    (2, 2), (1, 0), (0, 1), (3, 0), (0, 3), (2, 1), (1, 2), (2, 3),
    (3, 2), (1, 1), (3, 3), (2, 0), (0, 2), (1, 3), (3, 1),
)


def kernel(
    layers, flat, offsets, probes, tiles_out, check_out,
    stage, wide, to_tp, tile, column, features, total, other, gated, check,
    stage_sem, send_a, recv_a, send_b, recv_b, own_p, send_p, recv_p, send_f, recv_f,
    send_r, recv_r, send_h, recv_h, out_sem,
):
    tp = lax.axis_index("tp")
    grp = lax.axis_index("grp")
    core = lax.rem(tp, 2)
    z, x_lo, y = grp // 8, lax.rem(grp // 4, 2), lax.rem(grp, 4)
    mine = z * N_Y + y
    rows = to_tp.shape[4]
    blocks = to_tp.shape[3]
    chunks = tile.shape[0]
    per_layer = chunks // layers
    width = blocks * LANES
    tile_cols = per_layer * width
    tile_rows = tile.shape[3]
    half = other.shape[1]
    each = half // N_Q

    def peer(dz, dy):
        z2, y2 = lax.rem(z + dz, N_Z), lax.rem(y + dy, N_Y)
        return z2 * N_Y + y2, {"grp": z2 * 8 + x_lo * 4 + y2}

    def remote(src, dst, send, recv, where):
        return pltpu.make_async_remote_copy(
            src_ref=src, dst_ref=dst, send_sem=send, recv_sem=recv,
            device_id=where, device_id_type=MESH,
        )

    def drained(ref, sem):
        pltpu.make_async_copy(ref, ref, sem).wait()

    units = chunks * 2 * 4

    def unit_of(u):
        chunk, tensor, step = u // 8, lax.rem(u // 4, 2), lax.rem(u, 4)
        return chunk, tensor, step, lax.rem(tp + step + 1, 4)

    def fetch(u):
        chunk, tensor, step, dest = unit_of(u)
        start = dest * tile_cols + lax.rem(chunk, per_layer) * width
        slot = lax.rem(u, STAGES)
        return pltpu.make_async_copy(
            flat.at[chunk // per_layer, tensor, :, pl.ds(pl.multiple_of(start, LANES), width)],
            stage.at[slot], stage_sem.at[slot],
        )

    for u in range(STAGES):
        fetch(u).start()

    group = N_Y * each
    own = [
        pltpu.make_async_copy(
            probes.at[pl.ds((at * 2 + lo) * group, group)],
            features.at[mine, pl.ds(lo * half + at * group, group)],
            own_p.at[at * 2 + lo],
        )
        for at in range(N_Z) for lo in range(2)
    ]
    for copy in own:
        copy.start()
    for copy in own:
        copy.wait()
    share = pl.ds(pl.multiple_of(core * half, half), half)
    for dz, dy in STEPS:
        _, where = peer(dz, dy)
        remote(features.at[mine, share], features.at[mine, share], send_p, recv_p, where).start()

    def pick(u, _):
        chunk, tensor, step, dest = unit_of(u)
        slot = lax.rem(u, STAGES)
        fetch(u).wait()
        for block in range(blocks):
            wide[block] = stage[slot, :, block * LANES:(block + 1) * LANES].astype(jnp.float32)
        first = offsets[chunk // per_layer, tensor]

        @pl.when(step < 3)
        def _():
            for block in range(blocks):
                to_tp[chunk, tensor, step, block] = wide[
                    block, pl.ds(first, rows)
                ].astype(jnp.bfloat16)
            remote(
                to_tp.at[chunk, tensor, step],
                tile.at[chunk, :, tensor, pl.ds(pl.multiple_of(tp * rows, rows), rows)],
                send_a, recv_a.at[chunk], {"tp": dest},
            ).start()

        @pl.when(step == 3)
        def _():
            for block in range(blocks):
                tile[chunk, block, tensor, pl.ds(pl.multiple_of(tp * rows, rows), rows)] = wide[
                    block, pl.ds(first, rows)
                ].astype(jnp.bfloat16)

        @pl.when(u + STAGES < units)
        def _():
            fetch(u + STAGES).start()

        return 0

    lax.fori_loop(0, units, pick, 0)

    others = features.at[pl.ds(0, N_Q - 1), pl.ds(0, half)]
    drained(others, recv_p)
    neighbour = {"tp": tp + 1 - 2 * core}

    def hand_on(step, _):
        at = lax.rem(mine + step + 1, N_Q)
        remote(features.at[at, share], features.at[at, share], send_f, recv_f, neighbour).start()
        return 0

    lax.fori_loop(0, N_Q - 1, hand_on, 0)
    drained(others, recv_f)

    def spread(chunk):
        drained(to_tp.at[0], recv_a.at[chunk])
        for dz, dy in STEPS:
            at, where = peer(dz, dy)
            remote(tile.at[chunk, at], column.at[chunk, mine], send_b, recv_b.at[chunk], where).start()
        column[chunk, mine] = tile[chunk, mine]
        layer, part = chunk // per_layer, lax.rem(chunk, per_layer)

        def put(block, _):
            start = pl.multiple_of(part * width + block * LANES, LANES)
            for tensor in range(2):
                pltpu.make_async_copy(
                    tile.at[chunk, block, tensor],
                    tiles_out.at[layer, tensor, :, pl.ds(start, LANES)],
                    out_sem,
                ).start()
            return 0

        lax.fori_loop(0, blocks, put, 0)

    partner = {"grp": grp + 4 - 8 * x_lo}
    keep = pl.ds(pl.multiple_of(x_lo * half, half), half)
    give = pl.ds(pl.multiple_of((1 - x_lo) * half, half), half)

    def multiply(chunk):
        drained(column.at[chunk, pl.ds(0, N_Q - 1)], recv_b.at[chunk])
        total[chunk] = jnp.zeros(total.shape[1:], jnp.float32)

        def add(at, _):
            weights = jnp.concatenate([column[chunk, at, 0], column[chunk, at, 1]], axis=1)
            total[chunk] += jnp.dot(features[at], weights, preferred_element_type=jnp.float32)
            return 0

        lax.fori_loop(0, N_Q, add, 0)
        remote(total.at[chunk, give], other.at[chunk], send_r, recv_r.at[chunk], partner).start()

    def gate(chunk, _):
        drained(other.at[chunk], recv_r.at[chunk])
        sums = total[chunk, keep] + other[chunk]
        v, up = sums[:, :LANES], sums[:, LANES:]
        hidden = (v / (1.0 + jnp.exp(-v)) * up).astype(jnp.bfloat16)
        gated[chunk] = hidden.reshape(N_Q, each, LANES)
        check[mine, chunk] = gated[chunk, mine]
        for dz, dy in STEPS:
            at, where = peer(dz, dy)
            remote(gated.at[chunk, at], check.at[mine, chunk], send_h, recv_h, where).start()
        return 0

    spread(0)

    def step(chunk, _):
        spread(chunk)
        multiply(chunk - 1)
        return 0

    lax.fori_loop(1, chunks, step, 0)
    multiply(chunks - 1)
    lax.fori_loop(0, chunks, gate, 0)

    arrived = check.at[pl.ds(0, N_Q - 1)]
    drained(arrived, recv_h)
    for chunk in range(chunks):
        for at in range(N_Q):
            start = (chunk % per_layer) * width + at * LANES
            check_out[chunk // per_layer, :, start:start + LANES] = check[at, chunk]

    drained(to_tp, send_a)
    drained(column.at[:, pl.ds(0, N_Q - 1)], send_b)
    drained(others, send_p)
    drained(others, send_f)
    drained(other, send_r)
    drained(arrived, send_h)
    drained(tile, out_sem)


def per_device(flat_shards, offsets, probes):
    tp_count = lax.axis_size("tp")
    layers = flat_shards.shape[0]
    rows = flat_shards.shape[2] - PAD
    tile_cols = flat_shards.shape[3] // tp_count
    tile_rows = rows * tp_count
    count = probes.shape[0]
    half = count // 2
    each = half // N_Q
    width = N_Q * LANES
    chunks = layers * (tile_cols // width)
    bf16, f32 = jnp.bfloat16, jnp.float32
    dma = pltpu.SemaphoreType.DMA
    return pl.pallas_call(
        functools.partial(kernel, layers),
        out_shape=(
            jax.ShapeDtypeStruct((layers, 2, tile_rows, tile_cols), bf16),
            jax.ShapeDtypeStruct((layers, each, tile_cols), bf16),
        ),
        in_specs=[
            pl.BlockSpec(memory_space=pl.ANY),
            pl.BlockSpec(memory_space=pltpu.SMEM),
            pl.BlockSpec(memory_space=pl.ANY),
        ],
        out_specs=(pl.BlockSpec(memory_space=pl.ANY), pl.BlockSpec(memory_space=pltpu.VMEM)),
        scratch_shapes=[
            pltpu.VMEM((STAGES, rows + PAD, width), bf16),
            pltpu.VMEM((N_Q, rows + PAD, LANES), f32),
            pltpu.VMEM((chunks, 2, 3, N_Q, rows, LANES), bf16),
            pltpu.VMEM((chunks, N_Q, 2, tile_rows, LANES), bf16),
            pltpu.VMEM((chunks, N_Q, 2, tile_rows, LANES), bf16),
            pltpu.VMEM((N_Q, count, probes.shape[1]), bf16),
            pltpu.VMEM((chunks, count, 2 * LANES), f32),
            pltpu.VMEM((chunks, half, 2 * LANES), f32),
            pltpu.VMEM((chunks, N_Q, each, LANES), bf16),
            pltpu.VMEM((N_Q, chunks, each, LANES), bf16),
            dma((STAGES,)), dma, dma((chunks,)), dma, dma((chunks,)),
            dma((2 * N_Z,)), dma, dma, dma, dma,
            dma, dma((chunks,)), dma, dma, dma,
        ],
        compiler_params=pltpu.CompilerParams(has_side_effects=True, vmem_limit_bytes=62 * 2**20),
        name="reshard_check",
    )(flat_shards, offsets, probes)


def solution(mesh):
    placed = (P(None, None, ("grp", "tp"), None), P(), P(None, "grp"))
    return jax.shard_map(
        per_device,
        mesh=mesh,
        in_specs=placed,
        out_specs=(P(None, None, "grp", "tp"), P(None, "grp", "tp")),
        check_vma=False,
    )
```

time: 653 us -> 259 us (0.40)
  Pallas kernels: 0 us -> 228 us
  waiting for transfers between devices: 225 us -> 0 us
  local copies, waits for them, and re-layouts: 213 us -> 25.3 us
  blocking collectives: 167 us -> 0 us
  between operations: 21.3 us -> 0.65 us
  matrix products: 11.8 us -> 0 us
    pallas_call x0 -> x1, Pallas kernels: none -> 228 us  [per_device(): pl.pallas_call(functools.partial(kernel, layers), out_shape=(jax.ShapeDty...]
    all_to_all x1 -> x0, waiting for transfers between devices: 224 us -> none  [per_device(): lax.all_to_all(picked, 'tp', split_axis=4, concat_axis=2, tiled=True)]
    all_to_all x2 -> x0, blocking collectives: 167 us -> none  [the longest x1 151 us: per_device(): lax.all_to_all(split_tiles, 'grp', split_axis=3, concat_axis=2, tiled=True)]
    another operation x2 -> x0, local copies, waits for them, and re-layouts: 54.9 us -> none  [per_device(): serving_tiles.reshape(layer_count, 2, serving_tiles.shape[2], grp_count,...]
    reshape x3 -> x0, local copies, waits for them, and re-layouts: 51.8 us -> none  [the longest x2 32.3 us: per_device(): jnp.stack(picked_list)]
    slice x2 -> x0, local copies, waits for them, and re-layouts: 32.1 us -> none  [the longest x1 30.7 us: per_device(): flat_shards[which_layer, which_tensor]]
    all_to_all x5 -> x0, local copies, waits for them, and re-layouts: 29.5 us -> none  [the longest x1 17.2 us: per_device(): lax.all_to_all(split_tiles, 'grp', split_axis=3, concat_axis=2, tiled=True)]
    dynamic_slice x2 -> x0, local copies, waits for them, and re-layouts: 29.2 us -> none  [per_device(): lax.dynamic_slice_in_dim(flat_shards[which_layer, which_tensor], start, s...]
  transfers between devices with their start and end apart: 2 -> 0, of which waited for: 1 -> 0; matrix products, arithmetic and copies ran while one was open for 16% -> 0% of each run, Pallas kernels for 0% -> 0%
where the time goes in v1:
time: 259 us; the launch traced here: 254 us
  Pallas kernels  228 us (88%)
  local copies, waits for them, and re-layouts  25.3 us (10%)
    pallas_call x1, Pallas kernels, per_device(): pl.pallas_call(functools.partial(kernel, layers), out_shape=(jax.ShapeDty...  228 us
    unnamed x5, local copies, waits for them, and re-layouts  25.3 us

profile of v1, /device:TPU:0, one launch (start us, length us, event | category | flops | bytes accessed | tf_op | source)
XLA Modules:
  0.0 254.3 jit_solution(13608876648337748799)
XLA Ops:
  0.6 13.8 %copy.5.flat = bf16[2,2,66,24576]{3,2,1,0:T(8,128)(2,1)} copy(bf16[2,2,66,24576]{3,1,2,0:T(2,128)(2,1)} %param.3) | data formatting | bytes 25952256 | tf_op args[0]
  14.4 228.4 %reshard_check.1 = (bf16[2,2,256,6144]{3,2,1,0:T(8,128)(2,1)}, bf16[2,16,6144]{2,1,0:T(8,128)(2,1)}) custom-call(bf16[2,2,66,24576]{3,2,1,0:T(8,128)(2,1)} %copy.5.flat, s32[2,2]{1,0:T(2,128)} %offsets.1, bf16[512,256]{1,0:T(8,128)(2,1)} %probes.1), custom_call_target="tpu_custom_call" | custom-call | tf_op jit(solution)/shard_map/reshard_check/pallas_call | solution.py:229
  242.8 0.0 copy-start
  242.8 10.8 %copy.8 = bf16[2,2,256,6144]{3,2,1,0:T(8,128)(2,1)} copy(bf16[2,2,256,6144]{3,2,1,0:T(8,128)(2,1)} %get-tuple-element.4) | data formatting | bytes 25165824
  253.6 0.0 copy-done
  253.6 0.7 copy.9
Async XLA Ops:
  242.8 10.8 %copy-start = (bf16[2,16,6144]{2,1,0:T(8,128)(2,1)S(1)}, bf16[2,16,6144]{2,1,0:T(8,128)(2,1)}, u32[]{:S(2)}) copy-start(bf16[2,16,6144]{2,1,0:T(8,128)(2,1)} %get-tuple-element.5) | copy-start | bytes 1179652

commit v2 on v1

--- a/solution.py
+++ b/solution.py
@@ -13,6 +13,7 @@
 N_Z = 4
 N_Q = N_Y * N_Z
 STAGES = 4
+LAG = 3
 MESH = pl.DeviceIdType.MESH
 
 STEPS = (
@@ -24,7 +25,7 @@
 def kernel(
     layers, flat, offsets, probes, tiles_out, check_out,
     stage, wide, to_tp, tile, column, features, total, other, gated, check,
-    stage_sem, send_a, recv_a, send_b, recv_b, own_p, send_p, recv_p, send_f, recv_f,
+    stage_sem, send_a, recv_n, recv_a, send_b, recv_b, own_p, send_p, recv_p, send_f, recv_f,
     send_r, recv_r, send_h, recv_h, out_sem,
 ):
     tp = lax.axis_index("tp")
@@ -38,7 +39,7 @@
     per_layer = chunks // layers
     width = blocks * LANES
     tile_cols = per_layer * width
-    tile_rows = tile.shape[3]
+    pair = 2 * rows
     half = other.shape[1]
     each = half // N_Q
 
@@ -59,7 +60,9 @@
 
     def unit_of(u):
         chunk, tensor, step = u // 8, lax.rem(u // 4, 2), lax.rem(u, 4)
-        return chunk, tensor, step, lax.rem(tp + step + 1, 4)
+        far = 2 - 2 * (tp // 2) + lax.rem(core + step, 2)
+        near = 2 * (tp // 2) + lax.rem(core + step + 1, 2)
+        return chunk, tensor, step, jnp.where(step < 2, far, near)
 
     def fetch(u):
         chunk, tensor, step, dest = unit_of(u)
@@ -91,6 +94,13 @@
         _, where = peer(dz, dy)
         remote(features.at[mine, share], features.at[mine, share], send_p, recv_p, where).start()
 
+    def picked(block, first):
+        return wide[block, pl.ds(first, rows)].astype(jnp.bfloat16)
+
+    own_rows = pl.ds(pl.multiple_of(tp * rows, rows), rows)
+    near_rows = pl.ds(pl.multiple_of((tp // 2) * pair, pair), pair)
+    far_rows = pl.ds(pl.multiple_of((1 - tp // 2) * pair, pair), pair)
+
     def pick(u, _):
         chunk, tensor, step, dest = unit_of(u)
         slot = lax.rem(u, STAGES)
@@ -99,24 +109,26 @@
             wide[block] = stage[slot, :, block * LANES:(block + 1) * LANES].astype(jnp.float32)
         first = offsets[chunk // per_layer, tensor]
 
-        @pl.when(step < 3)
-        def _():
+        def send(recv):
             for block in range(blocks):
-                to_tp[chunk, tensor, step, block] = wide[
-                    block, pl.ds(first, rows)
-                ].astype(jnp.bfloat16)
+                to_tp[chunk, tensor, step, block] = picked(block, first)
             remote(
-                to_tp.at[chunk, tensor, step],
-                tile.at[chunk, :, tensor, pl.ds(pl.multiple_of(tp * rows, rows), rows)],
-                send_a, recv_a.at[chunk], {"tp": dest},
+                to_tp.at[chunk, tensor, step], tile.at[chunk, :, tensor, own_rows],
+                send_a, recv.at[chunk], {"tp": dest},
             ).start()
 
+        @pl.when(step < 2)
+        def _():
+            send(recv_a)
+
+        @pl.when(step == 2)
+        def _():
+            send(recv_n)
+
         @pl.when(step == 3)
         def _():
             for block in range(blocks):
-                tile[chunk, block, tensor, pl.ds(pl.multiple_of(tp * rows, rows), rows)] = wide[
-                    block, pl.ds(first, rows)
-                ].astype(jnp.bfloat16)
+                tile[chunk, block, tensor, own_rows] = picked(block, first)
 
         @pl.when(u + STAGES < units)
         def _():
@@ -124,7 +136,29 @@
 
         return 0
 
-    lax.fori_loop(0, units, pick, 0)
+    def spread(chunk, which):
+        for dz, dy in STEPS:
+            at, where = peer(dz, dy)
+            remote(
+                tile.at[chunk, at, :, which], column.at[chunk, mine, :, which],
+                send_b, recv_b.at[chunk], where,
+            ).start()
+
+    def spread_near(chunk):
+        drained(to_tp.at[0, :, 0], recv_n.at[chunk])
+        spread(chunk, near_rows)
+
+    def picks(chunk, _):
+        lax.fori_loop(chunk * 8, chunk * 8 + 8, pick, 0)
+
+        @pl.when(chunk > 0)
+        def _():
+            spread_near(chunk - 1)
+
+        return 0
+
+    lax.fori_loop(0, chunks, picks, 0)
+    spread_near(chunks - 1)
 
     others = features.at[pl.ds(0, N_Q - 1), pl.ds(0, half)]
     drained(others, recv_p)
@@ -138,11 +172,9 @@
     lax.fori_loop(0, N_Q - 1, hand_on, 0)
     drained(others, recv_f)
 
-    def spread(chunk):
-        drained(to_tp.at[0], recv_a.at[chunk])
-        for dz, dy in STEPS:
-            at, where = peer(dz, dy)
-            remote(tile.at[chunk, at], column.at[chunk, mine], send_b, recv_b.at[chunk], where).start()
+    def spread_far(chunk):
+        drained(to_tp.at[0, :, pl.ds(0, 2)], recv_a.at[chunk])
+        spread(chunk, far_rows)
         column[chunk, mine] = tile[chunk, mine]
         layer, part = chunk // per_layer, lax.rem(chunk, per_layer)
 
@@ -174,7 +206,7 @@
         lax.fori_loop(0, N_Q, add, 0)
         remote(total.at[chunk, give], other.at[chunk], send_r, recv_r.at[chunk], partner).start()
 
-    def gate(chunk, _):
+    def gate(chunk):
         drained(other.at[chunk], recv_r.at[chunk])
         sums = total[chunk, keep] + other[chunk]
         v, up = sums[:, :LANES], sums[:, LANES:]
@@ -184,18 +216,25 @@
         for dz, dy in STEPS:
             at, where = peer(dz, dy)
             remote(gated.at[chunk, at], check.at[mine, chunk], send_h, recv_h, where).start()
-        return 0
-
-    spread(0)
 
     def step(chunk, _):
-        spread(chunk)
-        multiply(chunk - 1)
-        return 0
-
-    lax.fori_loop(1, chunks, step, 0)
-    multiply(chunks - 1)
-    lax.fori_loop(0, chunks, gate, 0)
+        spread_far(chunk)
+
+        @pl.when(chunk >= LAG)
+        def _():
+            multiply(chunk - LAG)
+
+        return 0
+
+    def finish(chunk, _):
+        multiply(chunk)
+        gate(chunk - LAG)
+        return 0
+
+    lax.fori_loop(0, chunks, step, 0)
+    lax.fori_loop(chunks - LAG, chunks, finish, 0)
+    for chunk in range(chunks - LAG, chunks):
+        gate(chunk)
 
     arrived = check.at[pl.ds(0, N_Q - 1)]
     drained(arrived, recv_h)
@@ -249,7 +288,7 @@
             pltpu.VMEM((chunks, half, 2 * LANES), f32),
             pltpu.VMEM((chunks, N_Q, each, LANES), bf16),
             pltpu.VMEM((N_Q, chunks, each, LANES), bf16),
-            dma((STAGES,)), dma, dma((chunks,)), dma, dma((chunks,)),
+            dma((STAGES,)), dma, dma((chunks,)), dma((chunks,)), dma, dma((chunks,)),
             dma((2 * N_Z,)), dma, dma, dma, dma,
             dma, dma((chunks,)), dma, dma, dma,
         ],

time: 259 us -> 225 us (0.87); the launches traced: 254 us -> 224 us
  Pallas kernels: 228 us -> 198 us
    pallas_call x1, Pallas kernels: 228 us -> 198 us  [per_device(): pl.pallas_call(functools.partial(kernel, layers), out_shape=(jax.ShapeDty...]
where the time goes in v2:
time: 225 us; the launch traced here: 224 us
  Pallas kernels  198 us (88%)
  local copies, waits for them, and re-layouts  25.3 us (11%)
    pallas_call x1, Pallas kernels, per_device(): pl.pallas_call(functools.partial(kernel, layers), out_shape=(jax.ShapeDty...  198 us
    unnamed x5, local copies, waits for them, and re-layouts  25.3 us

profile of v2, /device:TPU:0, one launch (start us, length us, event | category | flops | bytes accessed | tf_op | source)
XLA Modules:
  0.0 224.4 jit_solution(10088656200702894503)
XLA Ops:
  0.6 13.8 %copy.5.flat = bf16[2,2,66,24576]{3,2,1,0:T(8,128)(2,1)} copy(bf16[2,2,66,24576]{3,1,2,0:T(2,128)(2,1)} %param.3) | data formatting | bytes 25952256 | tf_op args[0]
  14.4 198.4 %reshard_check.1 = (bf16[2,2,256,6144]{3,2,1,0:T(8,128)(2,1)}, bf16[2,16,6144]{2,1,0:T(8,128)(2,1)}) custom-call(bf16[2,2,66,24576]{3,2,1,0:T(8,128)(2,1)} %copy.5.flat, s32[2,2]{1,0:T(2,128)} %offsets.1, bf16[512,256]{1,0:T(8,128)(2,1)} %probes.1), custom_call_target="tpu_custom_call" | custom-call | tf_op jit(solution)/shard_map/reshard_check/pallas_call | solution.py:268
  212.8 0.0 copy-start
  212.8 10.8 %copy.8 = bf16[2,2,256,6144]{3,2,1,0:T(8,128)(2,1)} copy(bf16[2,2,256,6144]{3,2,1,0:T(8,128)(2,1)} %get-tuple-element.4) | data formatting | bytes 25165824
  223.6 0.0 copy-done
  223.6 0.7 copy.9
Async XLA Ops:
  212.8 10.8 %copy-start = (bf16[2,16,6144]{2,1,0:T(8,128)(2,1)S(1)}, bf16[2,16,6144]{2,1,0:T(8,128)(2,1)}, u32[]{:S(2)}) copy-start(bf16[2,16,6144]{2,1,0:T(8,128)(2,1)} %get-tuple-element.5) | copy-start | bytes 1179652

commit v3 on v2

--- a/solution.py
+++ b/solution.py
@@ -24,7 +24,7 @@
 
 def kernel(
     layers, flat, offsets, probes, tiles_out, check_out,
-    stage, wide, to_tp, tile, column, features, total, other, gated, check,
+    stage, to_tp, tile, column, features, total, other, gated, check,
     stage_sem, send_a, recv_n, recv_a, send_b, recv_b, own_p, send_p, recv_p, send_f, recv_f,
     send_r, recv_r, send_h, recv_h, out_sem,
 ):
@@ -56,20 +56,20 @@
     def drained(ref, sem):
         pltpu.make_async_copy(ref, ref, sem).wait()
 
-    units = chunks * 2 * 4
+    units = chunks * 4
 
     def unit_of(u):
-        chunk, tensor, step = u // 8, lax.rem(u // 4, 2), lax.rem(u, 4)
+        chunk, step = u // 4, lax.rem(u, 4)
         far = 2 - 2 * (tp // 2) + lax.rem(core + step, 2)
         near = 2 * (tp // 2) + lax.rem(core + step + 1, 2)
-        return chunk, tensor, step, jnp.where(step < 2, far, near)
+        return chunk, step, jnp.where(step < 2, far, near)
 
     def fetch(u):
-        chunk, tensor, step, dest = unit_of(u)
+        chunk, step, dest = unit_of(u)
         start = dest * tile_cols + lax.rem(chunk, per_layer) * width
         slot = lax.rem(u, STAGES)
         return pltpu.make_async_copy(
-            flat.at[chunk // per_layer, tensor, :, pl.ds(pl.multiple_of(start, LANES), width)],
+            flat.at[chunk // per_layer, :, :, pl.ds(pl.multiple_of(start, LANES), width)],
             stage.at[slot], stage_sem.at[slot],
         )
 
@@ -94,28 +94,42 @@
         _, where = peer(dz, dy)
         remote(features.at[mine, share], features.at[mine, share], send_p, recv_p, where).start()
 
-    def picked(block, first):
-        return wide[block, pl.ds(first, rows)].astype(jnp.bfloat16)
+    held = stage.shape[1]
+    row = lax.broadcasted_iota(jnp.int32, (pair, 2 * held), 0)
+    col = lax.broadcasted_iota(jnp.int32, (pair, 2 * held), 1)
 
     own_rows = pl.ds(pl.multiple_of(tp * rows, rows), rows)
     near_rows = pl.ds(pl.multiple_of((tp // 2) * pair, pair), pair)
     far_rows = pl.ds(pl.multiple_of((1 - tp // 2) * pair, pair), pair)
 
     def pick(u, _):
-        chunk, tensor, step, dest = unit_of(u)
+        chunk, step, dest = unit_of(u)
         slot = lax.rem(u, STAGES)
         fetch(u).wait()
-        for block in range(blocks):
-            wide[block] = stage[slot, :, block * LANES:(block + 1) * LANES].astype(jnp.float32)
-        first = offsets[chunk // per_layer, tensor]
+        layer = chunk // per_layer
+        wanted = jnp.where(row < rows, 2 * (row + offsets[layer, 0]), 2 * (row - rows + offsets[layer, 1]) + 1)
+        chosen = jnp.where(col == wanted, 1.0, 0.0).astype(jnp.bfloat16)
+
+        def picked(store):
+            for at in range(0, blocks, 2):
+                both = stage[slot, :, :, at * LANES:(at + 2) * LANES].reshape(2 * held, 2 * LANES)
+                out = jnp.dot(chosen, both, preferred_element_type=jnp.float32).astype(jnp.bfloat16)
+                for block in range(2):
+                    for tensor in range(2):
+                        store(at + block, tensor, out[
+                            tensor * rows:(tensor + 1) * rows, block * LANES:(block + 1) * LANES
+                        ])
 
         def send(recv):
-            for block in range(blocks):
-                to_tp[chunk, tensor, step, block] = picked(block, first)
-            remote(
-                to_tp.at[chunk, tensor, step], tile.at[chunk, :, tensor, own_rows],
-                send_a, recv.at[chunk], {"tp": dest},
-            ).start()
+            def store(block, tensor, value):
+                to_tp[chunk, tensor, step, block] = value
+
+            picked(store)
+            for tensor in range(2):
+                remote(
+                    to_tp.at[chunk, tensor, step], tile.at[chunk, :, tensor, own_rows],
+                    send_a, recv.at[chunk], {"tp": dest},
+                ).start()
 
         @pl.when(step < 2)
         def _():
@@ -127,8 +141,10 @@
 
         @pl.when(step == 3)
         def _():
-            for block in range(blocks):
-                tile[chunk, block, tensor, own_rows] = picked(block, first)
+            def store(block, tensor, value):
+                tile[chunk, block, tensor, own_rows] = value
+
+            picked(store)
 
         @pl.when(u + STAGES < units)
         def _():
@@ -149,7 +165,7 @@
         spread(chunk, near_rows)
 
     def picks(chunk, _):
-        lax.fori_loop(chunk * 8, chunk * 8 + 8, pick, 0)
+        lax.fori_loop(chunk * 4, chunk * 4 + 4, pick, 0)
 
         @pl.when(chunk > 0)
         def _():
@@ -278,8 +294,7 @@
         ],
         out_specs=(pl.BlockSpec(memory_space=pl.ANY), pl.BlockSpec(memory_space=pltpu.VMEM)),
         scratch_shapes=[
-            pltpu.VMEM((STAGES, rows + PAD, width), bf16),
-            pltpu.VMEM((N_Q, rows + PAD, LANES), f32),
+            pltpu.VMEM((STAGES, rows + PAD, 2, width), bf16),
             pltpu.VMEM((chunks, 2, 3, N_Q, rows, LANES), bf16),
             pltpu.VMEM((chunks, N_Q, 2, tile_rows, LANES), bf16),
             pltpu.VMEM((chunks, N_Q, 2, tile_rows, LANES), bf16),
@@ -294,7 +309,7 @@
         ],
         compiler_params=pltpu.CompilerParams(has_side_effects=True, vmem_limit_bytes=62 * 2**20),
         name="reshard_check",
-    )(flat_shards, offsets, probes)
+    )(jnp.transpose(flat_shards, (0, 2, 1, 3)), offsets, probes)
 
 
 def solution(mesh):

time: 225 us -> 211 us (0.938)
  local copies, waits for them, and re-layouts: 25.3 us -> 11.5 us
    unnamed x5 -> x4, local copies, waits for them, and re-layouts: 25.3 us -> 11.5 us
where the time goes in v3:
time: 211 us
  Pallas kernels  199 us (94%)
  local copies, waits for them, and re-layouts  11.5 us (5%)
    pallas_call x1, Pallas kernels, per_device(): pl.pallas_call(functools.partial(kernel, layers), out_shape=(jax.ShapeDty...  199 us
    unnamed x4, local copies, waits for them, and re-layouts  11.5 us

profile of v3, /device:TPU:0, one launch (start us, length us, event | category | flops | bytes accessed | tf_op | source)
XLA Modules:
  0.0 211.0 jit_solution(13982434896464905114)
XLA Ops:
  0.6 198.8 %reshard_check.1 = (bf16[2,2,256,6144]{3,2,1,0:T(8,128)(2,1)}, bf16[2,16,6144]{2,1,0:T(8,128)(2,1)}) custom-call(bf16[2,66,2,24576]{3,2,1,0:T(2,128)(2,1)} %bitcast.1, s32[2,2]{1,0:T(2,128)} %offsets.1, bf16[512,256]{1,0:T(8,128)(2,1)} %probes.1), custom_call_target="tpu_custom_call" | custom-call | tf_op jit(solution)/shard_map/reshard_check/pallas_call | solution.py:284
  199.4 0.0 copy-start
  199.4 10.8 %copy.7 = bf16[2,2,256,6144]{3,2,1,0:T(8,128)(2,1)} copy(bf16[2,2,256,6144]{3,2,1,0:T(8,128)(2,1)} %get-tuple-element.4) | data formatting | bytes 25165824
  210.2 0.0 copy-done
  210.2 0.7 copy.8
Async XLA Ops:
  199.4 10.8 %copy-start = (bf16[2,16,6144]{2,1,0:T(8,128)(2,1)S(1)}, bf16[2,16,6144]{2,1,0:T(8,128)(2,1)}, u32[]{:S(2)}) copy-start(bf16[2,16,6144]{2,1,0:T(8,128)(2,1)} %get-tuple-element.5) | copy-start | bytes 1179652

commit v4 on v3

--- a/solution.py
+++ b/solution.py
@@ -23,10 +23,10 @@
 
 
 def kernel(
-    layers, flat, offsets, probes, tiles_out, check_out,
-    stage, to_tp, tile, column, features, total, other, gated, check,
+    layers, flat, offsets, probes, tile, check,
+    stage, to_tp, column, features, total, other, gated,
     stage_sem, send_a, recv_n, recv_a, send_b, recv_b, own_p, send_p, recv_p, send_f, recv_f,
-    send_r, recv_r, send_h, recv_h, out_sem,
+    send_r, recv_r, send_h, recv_h,
 ):
     tp = lax.axis_index("tp")
     grp = lax.axis_index("grp")
@@ -56,6 +56,12 @@
     def drained(ref, sem):
         pltpu.make_async_copy(ref, ref, sem).wait()
 
+    barrier = pltpu.get_barrier_semaphore()
+    partner = {"grp": grp + 4 - 8 * x_lo}
+    met = [partner] + [{"tp": lax.rem(tp + by, 4)} for by in (1, 2, 3)] + [peer(dz, dy)[1] for dz, dy in STEPS]
+    for where in met:
+        pl.semaphore_signal(barrier, inc=1, device_id=where, device_id_type=MESH)
+
     units = chunks * 4
 
     def unit_of(u):
@@ -80,7 +86,7 @@
     own = [
         pltpu.make_async_copy(
             probes.at[pl.ds((at * 2 + lo) * group, group)],
-            features.at[mine, pl.ds(lo * half + at * group, group)],
+            features.at[z, y, pl.ds(lo * half + at * group, group)],
             own_p.at[at * 2 + lo],
         )
         for at in range(N_Z) for lo in range(2)
@@ -89,10 +95,28 @@
         copy.start()
     for copy in own:
         copy.wait()
+    pl.semaphore_wait(barrier, len(met))
     share = pl.ds(pl.multiple_of(core * half, half), half)
-    for dz, dy in STEPS:
-        _, where = peer(dz, dy)
-        remote(features.at[mine, share], features.at[mine, share], send_p, recv_p, where).start()
+    along_y = pl.ds(pl.multiple_of(core * half, half // 2), half // 2)
+    along_z = pl.ds(pl.multiple_of(core * half + half // 2, half // 2), half // 2)
+
+    def share_own():
+        for by in (2, 1, 3):
+            _, where_y = peer(0, by)
+            _, where_z = peer(by, 0)
+            for rows_of, where in ((along_y, where_y), (along_z, where_z)):
+                block = features.at[z, y, rows_of]
+                remote(block, block, send_p, recv_p.at[0], where).start()
+
+    def share_lines():
+        drained(features.at[0, pl.ds(0, 3), share], recv_p.at[0])
+        for by in (2, 1, 3):
+            _, where_y = peer(0, by)
+            _, where_z = peer(by, 0)
+            for line, where in ((features.at[z, :, along_y], where_z), (features.at[:, y, along_z], where_y)):
+                remote(line, line, send_p, recv_p.at[1], where).start()
+
+    share_own()
 
     held = stage.shape[1]
     row = lax.broadcasted_iota(jnp.int32, (pair, 2 * held), 0)
@@ -171,56 +195,54 @@
         def _():
             spread_near(chunk - 1)
 
+        @pl.when(chunk == 2)
+        def _():
+            share_lines()
+
         return 0
 
     lax.fori_loop(0, chunks, picks, 0)
     spread_near(chunks - 1)
 
-    others = features.at[pl.ds(0, N_Q - 1), pl.ds(0, half)]
-    drained(others, recv_p)
+    drained(features.at[pl.ds(0, 3), :, share], recv_p.at[1])
     neighbour = {"tp": tp + 1 - 2 * core}
 
     def hand_on(step, _):
         at = lax.rem(mine + step + 1, N_Q)
-        remote(features.at[at, share], features.at[at, share], send_f, recv_f, neighbour).start()
+        block = features.at[at // N_Y, lax.rem(at, N_Y), share]
+        remote(block, block, send_f, recv_f, neighbour).start()
         return 0
 
     lax.fori_loop(0, N_Q - 1, hand_on, 0)
+    others = column.at[0, pl.ds(0, N_Q - 1)]
     drained(others, recv_f)
 
     def spread_far(chunk):
         drained(to_tp.at[0, :, pl.ds(0, 2)], recv_a.at[chunk])
         spread(chunk, far_rows)
         column[chunk, mine] = tile[chunk, mine]
-        layer, part = chunk // per_layer, lax.rem(chunk, per_layer)
-
-        def put(block, _):
-            start = pl.multiple_of(part * width + block * LANES, LANES)
-            for tensor in range(2):
-                pltpu.make_async_copy(
-                    tile.at[chunk, block, tensor],
-                    tiles_out.at[layer, tensor, :, pl.ds(start, LANES)],
-                    out_sem,
-                ).start()
-            return 0
-
-        lax.fori_loop(0, blocks, put, 0)
-
-    partner = {"grp": grp + 4 - 8 * x_lo}
+
     keep = pl.ds(pl.multiple_of(x_lo * half, half), half)
     give = pl.ds(pl.multiple_of((1 - x_lo) * half, half), half)
 
     def multiply(chunk):
         drained(column.at[chunk, pl.ds(0, N_Q - 1)], recv_b.at[chunk])
-        total[chunk] = jnp.zeros(total.shape[1:], jnp.float32)
-
-        def add(at, _):
-            weights = jnp.concatenate([column[chunk, at, 0], column[chunk, at, 1]], axis=1)
-            total[chunk] += jnp.dot(features[at], weights, preferred_element_type=jnp.float32)
-            return 0
-
-        lax.fori_loop(0, N_Q, add, 0)
+
+        def product(part):
+            total[chunk, part] = jnp.zeros(other.shape[1:], jnp.float32)
+
+            def add(at, _):
+                weights = jnp.concatenate([column[chunk, at, 0], column[chunk, at, 1]], axis=1)
+                total[chunk, part] += jnp.dot(
+                    features[at // N_Y, lax.rem(at, N_Y), part], weights, preferred_element_type=jnp.float32
+                )
+                return 0
+
+            lax.fori_loop(0, N_Q, add, 0)
+
+        product(give)
         remote(total.at[chunk, give], other.at[chunk], send_r, recv_r.at[chunk], partner).start()
+        product(keep)
 
     def gate(chunk):
         drained(other.at[chunk], recv_r.at[chunk])
@@ -254,18 +276,31 @@
 
     arrived = check.at[pl.ds(0, N_Q - 1)]
     drained(arrived, recv_h)
-    for chunk in range(chunks):
-        for at in range(N_Q):
-            start = (chunk % per_layer) * width + at * LANES
-            check_out[chunk // per_layer, :, start:start + LANES] = check[at, chunk]
-
     drained(to_tp, send_a)
     drained(column.at[:, pl.ds(0, N_Q - 1)], send_b)
-    drained(others, send_p)
-    drained(others, send_f)
+    for sem in (send_p, send_f):
+        drained(others, sem)
     drained(other, send_r)
     drained(arrived, send_h)
-    drained(tile, out_sem)
+
+
+def place(tile, check, tiles_out, check_out, sem):
+    chunks, blocks = tile.shape[:2]
+    layers = tiles_out.shape[0]
+    per_layer = chunks // layers
+    copies = []
+    for chunk in range(chunks):
+        for block in range(blocks):
+            start = (chunk % per_layer * blocks + block) * LANES
+            for tensor in range(2):
+                copy = pltpu.make_async_copy(
+                    tile.at[chunk, block, tensor],
+                    tiles_out.at[chunk // per_layer, tensor, :, pl.ds(start, LANES)],
+                    sem,
+                )
+                copy.start()
+            check_out[chunk // per_layer, :, start:start + LANES] = check[block, chunk]
+    pltpu.make_async_copy(tile, tile, sem).wait()
 
 
 def per_device(flat_shards, offsets, probes):
@@ -281,35 +316,47 @@
     chunks = layers * (tile_cols // width)
     bf16, f32 = jnp.bfloat16, jnp.float32
     dma = pltpu.SemaphoreType.DMA
-    return pl.pallas_call(
+    tile, check = pl.pallas_call(
         functools.partial(kernel, layers),
         out_shape=(
-            jax.ShapeDtypeStruct((layers, 2, tile_rows, tile_cols), bf16),
-            jax.ShapeDtypeStruct((layers, each, tile_cols), bf16),
+            pltpu.VMEM((chunks, N_Q, 2, tile_rows, LANES), bf16),
+            pltpu.VMEM((N_Q, chunks, each, LANES), bf16),
         ),
         in_specs=[
             pl.BlockSpec(memory_space=pl.ANY),
             pl.BlockSpec(memory_space=pltpu.SMEM),
             pl.BlockSpec(memory_space=pl.ANY),
         ],
-        out_specs=(pl.BlockSpec(memory_space=pl.ANY), pl.BlockSpec(memory_space=pltpu.VMEM)),
+        out_specs=(pl.BlockSpec(memory_space=pltpu.VMEM), pl.BlockSpec(memory_space=pltpu.VMEM)),
         scratch_shapes=[
             pltpu.VMEM((STAGES, rows + PAD, 2, width), bf16),
             pltpu.VMEM((chunks, 2, 3, N_Q, rows, LANES), bf16),
             pltpu.VMEM((chunks, N_Q, 2, tile_rows, LANES), bf16),
-            pltpu.VMEM((chunks, N_Q, 2, tile_rows, LANES), bf16),
-            pltpu.VMEM((N_Q, count, probes.shape[1]), bf16),
+            pltpu.VMEM((N_Z, N_Y, count, probes.shape[1]), bf16),
             pltpu.VMEM((chunks, count, 2 * LANES), f32),
             pltpu.VMEM((chunks, half, 2 * LANES), f32),
             pltpu.VMEM((chunks, N_Q, each, LANES), bf16),
-            pltpu.VMEM((N_Q, chunks, each, LANES), bf16),
             dma((STAGES,)), dma, dma((chunks,)), dma((chunks,)), dma, dma((chunks,)),
-            dma((2 * N_Z,)), dma, dma, dma, dma,
-            dma, dma((chunks,)), dma, dma, dma,
+            dma((2 * N_Z,)), dma, dma((2,)), dma, dma,
+            dma, dma((chunks,)), dma, dma,
         ],
-        compiler_params=pltpu.CompilerParams(has_side_effects=True, vmem_limit_bytes=62 * 2**20),
+        compiler_params=pltpu.CompilerParams(
+            collective_id=0, has_side_effects=True, vmem_limit_bytes=51 * 2**20
+        ),
         name="reshard_check",
     )(jnp.transpose(flat_shards, (0, 2, 1, 3)), offsets, probes)
+    return pl.pallas_call(
+        place,
+        out_shape=(
+            jax.ShapeDtypeStruct((layers, 2, tile_rows, tile_cols), bf16),
+            jax.ShapeDtypeStruct((layers, each, tile_cols), bf16),
+        ),
+        in_specs=[pl.BlockSpec(memory_space=pltpu.VMEM), pl.BlockSpec(memory_space=pltpu.VMEM)],
+        out_specs=(pl.BlockSpec(memory_space=pl.ANY), pl.BlockSpec(memory_space=pltpu.VMEM)),
+        scratch_shapes=[dma],
+        compiler_params=pltpu.CompilerParams(vmem_limit_bytes=16 * 2**20),
+        name="place",
+    )(tile, check)
 
 
 def solution(mesh):

time: 211 us -> 189 us (0.90)
  local copies, waits for them, and re-layouts: 11.5 us -> 0 us
  Pallas kernels: 199 us -> 188 us
    unnamed x4 -> x0, local copies, waits for them, and re-layouts: 11.5 us -> none
    pallas_call x1 -> x2, Pallas kernels: 199 us -> 188 us  [the longest x1 183 us: per_device(): pl.pallas_call(functools.partial(kernel, layers), out_shape=(pltpu.VMEM((...]
where the time goes in v4:
time: 189 us
  Pallas kernels  188 us (99%)
    pallas_call x1, Pallas kernels, per_device(): pl.pallas_call(functools.partial(kernel, layers), out_shape=(pltpu.VMEM((...  183 us
    pallas_call x1, Pallas kernels, per_device(): pl.pallas_call(place, out_shape=(jax.ShapeDtypeStruct((layers, 2, tile_ro...  5.21 us

profile of v4, /device:TPU:0, one launch (start us, length us, event | category | flops | bytes accessed | tf_op | source)
XLA Modules:
  0.0 189.1 jit_solution(2514296941677342193)
XLA Ops:
  0.6 183.3 %reshard_check.1 = (bf16[6,16,2,256,128]{4,3,2,1,0:T(8,128)(2,1)S(1)}, bf16[16,6,16,128]{3,2,1,0:T(8,128)(2,1)S(1)}) custom-call(bf16[2,66,2,24576]{3,2,1,0:T(2,128)(2,1)} %bitcast.1, s32[2,2]{1,0:T(2,128)} %offsets.1, bf16[512,256]{1,0:T(8,128)(2,1)} %probes.1), custom_call_target="tpu_custom_call" | custom-call | tf_op jit(solution)/shard_map/reshard_check/pallas_call | solution.py:319
  183.9 5.2 %place.1 = (bf16[2,2,256,6144]{3,2,1,0:T(8,128)(2,1)}, bf16[2,16,6144]{2,1,0:T(8,128)(2,1)}) custom-call(bf16[6,16,2,256,128]{4,3,2,1,0:T(8,128)(2,1)S(1)} %get-tuple-element.4.tile, bf16[16,6,16,128]{3,2,1,0:T(8,128)(2,1)S(1)} %get-tuple-element.5.check), custom_call_target="tpu_custom_call" | custom-call | tf_op jit(solution)/shard_map/place/pallas_call | solution.py:348

commit v5 on v4

--- a/solution.py
+++ b/solution.py
@@ -93,9 +93,6 @@
     ]
     for copy in own:
         copy.start()
-    for copy in own:
-        copy.wait()
-    pl.semaphore_wait(barrier, len(met))
     share = pl.ds(pl.multiple_of(core * half, half), half)
     along_y = pl.ds(pl.multiple_of(core * half, half // 2), half // 2)
     along_z = pl.ds(pl.multiple_of(core * half + half // 2, half // 2), half // 2)
@@ -116,8 +113,6 @@
             for line, where in ((features.at[z, :, along_y], where_z), (features.at[:, y, along_z], where_y)):
                 remote(line, line, send_p, recv_p.at[1], where).start()
 
-    share_own()
-
     held = stage.shape[1]
     row = lax.broadcasted_iota(jnp.int32, (pair, 2 * held), 0)
     col = lax.broadcasted_iota(jnp.int32, (pair, 2 * held), 1)
@@ -126,7 +121,7 @@
     near_rows = pl.ds(pl.multiple_of((tp // 2) * pair, pair), pair)
     far_rows = pl.ds(pl.multiple_of((1 - tp // 2) * pair, pair), pair)
 
-    def pick(u, _):
+    def pick(u):
         chunk, step, dest = unit_of(u)
         slot = lax.rem(u, STAGES)
         fetch(u).wait()
@@ -144,11 +139,28 @@
                             tensor * rows:(tensor + 1) * rows, block * LANES:(block + 1) * LANES
                         ])
 
-        def send(recv):
+        @pl.when(step < 3)
+        def _():
             def store(block, tensor, value):
                 to_tp[chunk, tensor, step, block] = value
 
             picked(store)
+
+        @pl.when(step == 3)
+        def _():
+            def store(block, tensor, value):
+                tile[chunk, block, tensor, own_rows] = value
+
+            picked(store)
+
+        @pl.when(u + STAGES < units)
+        def _():
+            fetch(u + STAGES).start()
+
+    def ship(u, _):
+        chunk, step, dest = unit_of(u)
+
+        def send(recv):
             for tensor in range(2):
                 remote(
                     to_tp.at[chunk, tensor, step], tile.at[chunk, :, tensor, own_rows],
@@ -163,16 +175,9 @@
         def _():
             send(recv_n)
 
-        @pl.when(step == 3)
-        def _():
-            def store(block, tensor, value):
-                tile[chunk, block, tensor, own_rows] = value
-
-            picked(store)
-
-        @pl.when(u + STAGES < units)
-        def _():
-            fetch(u + STAGES).start()
+        @pl.when(u + 1 < units)
+        def _():
+            pick(u + 1)
 
         return 0
 
@@ -189,7 +194,7 @@
         spread(chunk, near_rows)
 
     def picks(chunk, _):
-        lax.fori_loop(chunk * 4, chunk * 4 + 4, pick, 0)
+        lax.fori_loop(chunk * 4, chunk * 4 + 4, ship, 0)
 
         @pl.when(chunk > 0)
         def _():
@@ -201,6 +206,11 @@
 
         return 0
 
+    pick(0)
+    for copy in own:
+        copy.wait()
+    pl.semaphore_wait(barrier, len(met))
+    share_own()
     lax.fori_loop(0, chunks, picks, 0)
     spread_near(chunks - 1)
 
@@ -228,21 +238,21 @@
     def multiply(chunk):
         drained(column.at[chunk, pl.ds(0, N_Q - 1)], recv_b.at[chunk])
 
-        def product(part):
-            total[chunk, part] = jnp.zeros(other.shape[1:], jnp.float32)
-
-            def add(at, _):
-                weights = jnp.concatenate([column[chunk, at, 0], column[chunk, at, 1]], axis=1)
-                total[chunk, part] += jnp.dot(
-                    features[at // N_Y, lax.rem(at, N_Y), part], weights, preferred_element_type=jnp.float32
-                )
-                return 0
-
-            lax.fori_loop(0, N_Q, add, 0)
-
-        product(give)
-        remote(total.at[chunk, give], other.at[chunk], send_r, recv_r.at[chunk], partner).start()
-        product(keep)
+        def product(turn, _):
+            part = pl.ds(pl.multiple_of(lax.rem(1 - x_lo + turn, 2) * half, half), half)
+            left = jnp.concatenate([features[at // N_Y, at % N_Y, part] for at in range(N_Q)], axis=1)
+            right = jnp.concatenate([
+                jnp.concatenate([column[chunk, at, 0], column[chunk, at, 1]], axis=1) for at in range(N_Q)
+            ], axis=0)
+            total[chunk, part] = jnp.dot(left, right, preferred_element_type=jnp.float32)
+
+            @pl.when(turn == 0)
+            def _():
+                remote(total.at[chunk, give], other.at[chunk], send_r, recv_r.at[chunk], partner).start()
+
+            return 0
+
+        lax.fori_loop(0, 2, product, 0)
 
     def gate(chunk):
         drained(other.at[chunk], recv_r.at[chunk])
@@ -284,11 +294,10 @@
     drained(arrived, send_h)
 
 
-def place(tile, check, tiles_out, check_out, sem):
+def place(tile, check, tiles_out, check_out, lines, sem, line_sem):
     chunks, blocks = tile.shape[:2]
     layers = tiles_out.shape[0]
     per_layer = chunks // layers
-    copies = []
     for chunk in range(chunks):
         for block in range(blocks):
             start = (chunk % per_layer * blocks + block) * LANES
@@ -299,7 +308,10 @@
                     sem,
                 )
                 copy.start()
-            check_out[chunk // per_layer, :, start:start + LANES] = check[block, chunk]
+            lines[chunk // per_layer, :, start:start + LANES] = check[block, chunk]
+    copy = pltpu.make_async_copy(lines, check_out, line_sem)
+    copy.start()
+    copy.wait()
     pltpu.make_async_copy(tile, tile, sem).wait()
 
 
@@ -352,8 +364,8 @@
             jax.ShapeDtypeStruct((layers, each, tile_cols), bf16),
         ),
         in_specs=[pl.BlockSpec(memory_space=pltpu.VMEM), pl.BlockSpec(memory_space=pltpu.VMEM)],
-        out_specs=(pl.BlockSpec(memory_space=pl.ANY), pl.BlockSpec(memory_space=pltpu.VMEM)),
-        scratch_shapes=[dma],
+        out_specs=(pl.BlockSpec(memory_space=pl.ANY), pl.BlockSpec(memory_space=pl.ANY)),
+        scratch_shapes=[pltpu.VMEM((layers, each, tile_cols), bf16), dma, dma],
         compiler_params=pltpu.CompilerParams(vmem_limit_bytes=16 * 2**20),
         name="place",
     )(tile, check)

time: 189 us -> 188 us (level)
  no operation moved by 1% of the time
where the time goes in v5:
time: 188 us
  Pallas kernels  188 us (100%)
    pallas_call x1, Pallas kernels, per_device(): pl.pallas_call(functools.partial(kernel, layers), out_shape=(pltpu.VMEM((...  183 us
    pallas_call x1, Pallas kernels, per_device(): pl.pallas_call(place, out_shape=(jax.ShapeDtypeStruct((layers, 2, tile_ro...  4.61 us

profile of v5, /device:TPU:0, one launch (start us, length us, event | category | flops | bytes accessed | tf_op | source)
XLA Modules:
  0.0 188.2 jit_solution(6429329290491043682)
XLA Ops:
  0.6 182.9 %reshard_check.1 = (bf16[6,16,2,256,128]{4,3,2,1,0:T(8,128)(2,1)S(1)}, bf16[16,6,16,128]{3,2,1,0:T(8,128)(2,1)S(1)}) custom-call(bf16[2,66,2,24576]{3,2,1,0:T(2,128)(2,1)} %bitcast.1, s32[2,2]{1,0:T(2,128)} %offsets.1, bf16[512,256]{1,0:T(8,128)(2,1)} %probes.1), custom_call_target="tpu_custom_call" | custom-call | tf_op jit(solution)/shard_map/reshard_check/pallas_call | solution.py:331
  183.5 4.6 %place.1 = (bf16[2,2,256,6144]{3,2,1,0:T(8,128)(2,1)}, bf16[2,16,6144]{2,1,0:T(8,128)(2,1)}) custom-call(bf16[6,16,2,256,128]{4,3,2,1,0:T(8,128)(2,1)S(1)} %get-tuple-element.4.tile, bf16[16,6,16,128]{3,2,1,0:T(8,128)(2,1)S(1)} %get-tuple-element.5.check), custom_call_target="tpu_custom_call" | custom-call | tf_op jit(solution)/shard_map/place/pallas_call | solution.py:360

commit v6 on v5

--- a/solution.py
+++ b/solution.py
@@ -24,9 +24,9 @@
 
 def kernel(
     layers, flat, offsets, probes, tile, check,
-    stage, to_tp, column, features, total, other, gated,
+    stage, to_tp, column, features, total, other, gated, ends,
     stage_sem, send_a, recv_n, recv_a, send_b, recv_b, own_p, send_p, recv_p, send_f, recv_f,
-    send_r, recv_r, send_h, recv_h,
+    send_r, recv_r, send_h, recv_h, send_e, recv_e,
 ):
     tp = lax.axis_index("tp")
     grp = lax.axis_index("grp")
@@ -58,7 +58,10 @@
 
     barrier = pltpu.get_barrier_semaphore()
     partner = {"grp": grp + 4 - 8 * x_lo}
-    met = [partner] + [{"tp": lax.rem(tp + by, 4)} for by in (1, 2, 3)] + [peer(dz, dy)[1] for dz, dy in STEPS]
+    met = [partner] + [{"tp": lax.rem(tp + by, 4)} for by in (1, 2, 3)]
+    for dz, dy in STEPS:
+        where = peer(dz, dy)[1]["grp"]
+        met += [{"grp": where}, {"grp": where + 4 - 8 * x_lo}]
     for where in met:
         pl.semaphore_signal(barrier, inc=1, device_id=where, device_id_type=MESH)
 
@@ -246,20 +249,41 @@
             ], axis=0)
             total[chunk, part] = jnp.dot(left, right, preferred_element_type=jnp.float32)
 
-            @pl.when(turn == 0)
+            @pl.when((turn == 0) & (chunk < chunks - 1))
             def _():
                 remote(total.at[chunk, give], other.at[chunk], send_r, recv_r.at[chunk], partner).start()
 
+            @pl.when((turn == 0) & (chunk == chunks - 1))
+            def _():
+                for dz, dy in STEPS + ((0, 0),):
+                    at, where = peer(dz, dy)
+                    remote(
+                        total.at[chunk, rows_for(1 - x_lo, at)], ends.at[x_lo * N_Q + mine],
+                        send_e, recv_e, {"grp": where["grp"] + 4 - 8 * x_lo},
+                    ).start()
+
+            @pl.when((turn == 1) & (chunk == chunks - 1))
+            def _():
+                for dz, dy in STEPS:
+                    at, where = peer(dz, dy)
+                    remote(
+                        total.at[chunk, rows_for(x_lo, at)], ends.at[x_lo * N_Q + mine], send_e, recv_e, where,
+                    ).start()
+
             return 0
 
         lax.fori_loop(0, 2, product, 0)
+
+    def rows_for(lo, at):
+        return pl.ds(pl.multiple_of(lo * half + at * each, each), each)
+
+    def gate_of(sums):
+        v, up = sums[..., :LANES], sums[..., LANES:]
+        return (v / (1.0 + jnp.exp(-v)) * up).astype(jnp.bfloat16)
 
     def gate(chunk):
         drained(other.at[chunk], recv_r.at[chunk])
-        sums = total[chunk, keep] + other[chunk]
-        v, up = sums[:, :LANES], sums[:, LANES:]
-        hidden = (v / (1.0 + jnp.exp(-v)) * up).astype(jnp.bfloat16)
-        gated[chunk] = hidden.reshape(N_Q, each, LANES)
+        gated[chunk] = gate_of(total[chunk, keep] + other[chunk]).reshape(N_Q, each, LANES)
         check[mine, chunk] = gated[chunk, mine]
         for dz, dy in STEPS:
             at, where = peer(dz, dy)
@@ -281,16 +305,23 @@
 
     lax.fori_loop(0, chunks, step, 0)
     lax.fori_loop(chunks - LAG, chunks, finish, 0)
-    for chunk in range(chunks - LAG, chunks):
+    for chunk in range(chunks - LAG, chunks - 1):
         gate(chunk)
-
-    arrived = check.at[pl.ds(0, N_Q - 1)]
+    ends[x_lo * N_Q + mine] = total[chunks - 1, rows_for(x_lo, mine)]
+    came = ends.at[pl.ds(0, 2 * N_Q - 1)]
+    drained(came, recv_e)
+    last = gate_of(ends[:N_Q] + ends[N_Q:])
+    for at in range(N_Q):
+        check[at, chunks - 1] = last[at]
+
+    arrived = check.at[pl.ds(0, N_Q - 1), pl.ds(0, chunks - 1)]
     drained(arrived, recv_h)
     drained(to_tp, send_a)
     drained(column.at[:, pl.ds(0, N_Q - 1)], send_b)
     for sem in (send_p, send_f):
         drained(others, sem)
-    drained(other, send_r)
+    drained(other.at[pl.ds(0, chunks - 1)], send_r)
+    drained(came, send_e)
     drained(arrived, send_h)
 
 
@@ -348,9 +379,10 @@
             pltpu.VMEM((chunks, count, 2 * LANES), f32),
             pltpu.VMEM((chunks, half, 2 * LANES), f32),
             pltpu.VMEM((chunks, N_Q, each, LANES), bf16),
+            pltpu.VMEM((2 * N_Q, each, 2 * LANES), f32),
             dma((STAGES,)), dma, dma((chunks,)), dma((chunks,)), dma, dma((chunks,)),
             dma((2 * N_Z,)), dma, dma((2,)), dma, dma,
-            dma, dma((chunks,)), dma, dma,
+            dma, dma((chunks,)), dma, dma, dma, dma,
         ],
         compiler_params=pltpu.CompilerParams(
             collective_id=0, has_side_effects=True, vmem_limit_bytes=51 * 2**20

time: 188 us -> 185 us (0.984)
  Pallas kernels: 188 us -> 184 us
    pallas_call x1, Pallas kernels: 183 us -> 179 us  [per_device(): pl.pallas_call(functools.partial(kernel, layers), out_shape=(pltpu.VMEM((...]
where the time goes in v6:
time: 185 us
  Pallas kernels  184 us (99%)
    pallas_call x1, Pallas kernels, per_device(): pl.pallas_call(functools.partial(kernel, layers), out_shape=(pltpu.VMEM((...  179 us
    pallas_call x1, Pallas kernels, per_device(): pl.pallas_call(place, out_shape=(jax.ShapeDtypeStruct((layers, 2, tile_ro...  4.61 us

profile of v6, /device:TPU:0, one launch (start us, length us, event | category | flops | bytes accessed | tf_op | source)
XLA Modules:
  0.0 184.6 jit_solution(5860589737797535526)
XLA Ops:
  0.6 179.3 %reshard_check.1 = (bf16[6,16,2,256,128]{4,3,2,1,0:T(8,128)(2,1)S(1)}, bf16[16,6,16,128]{3,2,1,0:T(8,128)(2,1)S(1)}) custom-call(bf16[2,66,2,24576]{3,2,1,0:T(2,128)(2,1)} %bitcast.1, s32[2,2]{1,0:T(2,128)} %offsets.1, bf16[512,256]{1,0:T(8,128)(2,1)} %probes.1), custom_call_target="tpu_custom_call" | custom-call | tf_op jit(solution)/shard_map/reshard_check/pallas_call | solution.py:362
  180.0 4.6 %place.1 = (bf16[2,2,256,6144]{3,2,1,0:T(8,128)(2,1)}, bf16[2,16,6144]{2,1,0:T(8,128)(2,1)}) custom-call(bf16[6,16,2,256,128]{4,3,2,1,0:T(8,128)(2,1)S(1)} %get-tuple-element.4.tile, bf16[16,6,16,128]{3,2,1,0:T(8,128)(2,1)S(1)} %get-tuple-element.5.check), custom_call_target="tpu_custom_call" | custom-call | tf_op jit(solution)/shard_map/place/pallas_call | solution.py:392

commit v7 on v6

--- a/solution.py
+++ b/solution.py
@@ -332,6 +332,12 @@
     for chunk in range(chunks):
         for block in range(blocks):
             start = (chunk % per_layer * blocks + block) * LANES
+            lines[chunk // per_layer, :, start:start + LANES] = check[block, chunk]
+    small = pltpu.make_async_copy(lines, check_out, line_sem)
+    small.start()
+    for chunk in range(chunks):
+        for block in range(blocks):
+            start = (chunk % per_layer * blocks + block) * LANES
             for tensor in range(2):
                 copy = pltpu.make_async_copy(
                     tile.at[chunk, block, tensor],
@@ -339,10 +345,7 @@
                     sem,
                 )
                 copy.start()
-            lines[chunk // per_layer, :, start:start + LANES] = check[block, chunk]
-    copy = pltpu.make_async_copy(lines, check_out, line_sem)
-    copy.start()
-    copy.wait()
+    small.wait()
     pltpu.make_async_copy(tile, tile, sem).wait()
 
 

time: 185 us -> 185 us (level)
  no operation moved by 1% of the time
where the time goes in v7:
time: 185 us
  Pallas kernels  184 us (99%)
    pallas_call x1, Pallas kernels, per_device(): pl.pallas_call(functools.partial(kernel, layers), out_shape=(pltpu.VMEM((...  179 us
    pallas_call x1, Pallas kernels, per_device(): pl.pallas_call(place, out_shape=(jax.ShapeDtypeStruct((layers, 2, tile_ro...  4.59 us

profile of v7, /device:TPU:0, one launch (start us, length us, event | category | flops | bytes accessed | tf_op | source)
XLA Modules:
  0.0 184.6 jit_solution(1474597496808473223)
XLA Ops:
  0.6 179.3 %reshard_check.1 = (bf16[6,16,2,256,128]{4,3,2,1,0:T(8,128)(2,1)S(1)}, bf16[16,6,16,128]{3,2,1,0:T(8,128)(2,1)S(1)}) custom-call(bf16[2,66,2,24576]{3,2,1,0:T(2,128)(2,1)} %bitcast.1, s32[2,2]{1,0:T(2,128)} %offsets.1, bf16[512,256]{1,0:T(8,128)(2,1)} %probes.1), custom_call_target="tpu_custom_call" | custom-call | tf_op jit(solution)/shard_map/reshard_check/pallas_call | solution.py:365
  180.0 4.6 %place.1 = (bf16[2,2,256,6144]{3,2,1,0:T(8,128)(2,1)}, bf16[2,16,6144]{2,1,0:T(8,128)(2,1)}) custom-call(bf16[6,16,2,256,128]{4,3,2,1,0:T(8,128)(2,1)S(1)} %get-tuple-element.4.tile, bf16[16,6,16,128]{3,2,1,0:T(8,128)(2,1)S(1)} %get-tuple-element.5.check), custom_call_target="tpu_custom_call" | custom-call | tf_op jit(solution)/shard_map/place/pallas_call | solution.py:395
